TPU v7x, 32 devices: a whole 2x2x4 slice. The times are simulated.
32 devices in a mesh: zero: 4 (over z), tp: 4 (over x, core), shift: 2 (over y).
Axes of the slice: x: 2, y: 2, z: 4, core: 2. Of those that a mesh axis runs over, the one named last changes fastest.
Arguments:
- train_gate: bfloat16 [4096, 8192], P(('shift', 'zero'), 'tp'), parts along dimension 0, may hold values from -0.125 to 0.125
- low_gate: bfloat16 [4096, 32], P(('shift', 'zero')), parts along dimension 0, may hold values from -0.125 to 0.125
- high_gate: bfloat16 [64, 8192], P('shift', 'tp'), parts along dimension 0, may hold values from -1 to 1
- train_up: bfloat16 [4096, 8192], P(('shift', 'zero'), 'tp'), parts along dimension 0, may hold values from -0.125 to 0.125
- low_up: bfloat16 [4096, 32], P(('shift', 'zero')), parts along dimension 0, may hold values from -0.125 to 0.125
- high_up: bfloat16 [64, 8192], P('shift', 'tp'), parts along dimension 0, may hold values from -1 to 1
- norm_train: float32 [4096], P(('shift', 'zero', 'tp')), parts along dimension 0, may hold values from 0.25 to 1.75
- norm_step: float32 [4096], P(('shift', 'zero', 'tp')), parts along dimension 0, may hold values from -0.3 to 0.3
Outputs:
- ready_gate: bfloat16 [16384, 2048], P(('shift', 'tp')), parts along dimension 0
- ready_up: bfloat16 [16384, 2048], P(('shift', 'tp')), parts along dimension 0
- serve_norm: bfloat16 [4096], P('shift'), parts along dimension 0
There are 2 independent parts, one for each index of `shift`. A program takes and returns all parts, laid end to end along the dimension named above; each array names one. Nothing has to cross between parts.
All inputs are finite; a program needn't handle non-finite values.
Results may differ from a plain program's by a relative error of at most 0.001.
Values may be sent and summed in bfloat16 or wider, within the bound.
A program may use at most 64 MiB of HBM per device.

v0:
```python
import jax
import jax.numpy as jnp
from jax import lax
from jax.sharding import PartitionSpec as P

mix_rate = 0.5


def body(train_gate, low_gate, high_gate, train_up, low_up, high_up, norm_train, norm_step):
    latest_gate = train_gate.astype(jnp.float32) + mix_rate * jnp.dot(
        low_gate, high_gate, preferred_element_type=jnp.float32
    )
    latest_up = train_up.astype(jnp.float32) + mix_rate * jnp.dot(
        low_up, high_up, preferred_element_type=jnp.float32
    )
    narrow_gate, narrow_up = (latest_gate.astype(jnp.bfloat16), latest_up.astype(jnp.bfloat16))
    ready_gate, ready_up = (
        lax.all_gather(narrow_gate, "zero", axis=0, tiled=True),
        lax.all_gather(narrow_up, "zero", axis=0, tiled=True),
    )
    ready_gate, ready_up = (ready_gate.T, ready_up.T)
    serve_norm = lax.all_gather(
        (norm_train + norm_step).astype(jnp.bfloat16), ("zero", "tp"), axis=0, tiled=True
    )
    return (ready_gate, ready_up, serve_norm)


def solution(mesh):
    in_specs = (
        P(("shift", "zero"), "tp"),
        P(("shift", "zero"), None),
        P("shift", "tp"),
        P(("shift", "zero"), "tp"),
        P(("shift", "zero"), None),
        P("shift", "tp"),
        P(("shift", "zero", "tp")),
        P(("shift", "zero", "tp")),
    )
    out_specs = (P(("shift", "tp"), None), P(("shift", "tp"), None), P("shift"))
    return jax.shard_map(body, mesh=mesh, in_specs=in_specs, out_specs=out_specs, check_vma=False)
```

profile of v0, /device:TPU:0, one launch (start us, length us, event | category | flops | bytes accessed | tf_op | source)
XLA Modules:
  0.0 332.7 jit_solution(4366362364971424566)
XLA Ops:
  7.2 0.0 copy-start
  7.2 0.0 copy-start.1
  7.2 0.0 copy-start.3
  7.2 0.0 copy-start.2
  7.2 0.0 all-gather.4.cloned.1.call-start
  7.3 0.8 copy-done
  8.1 3.7 %add_convert_fusion.1 = bf16[512,2048]{1,0:T(8,128)(2,1)} fusion(bf16[512,2048]{1,0:T(8,128)(2,1)} %param.8, bf16[512,32]{0,1:T(8,128)(2,1)} %param.9, bf16[32,2048]{1,0:T(8,128)(2,1)S(1)} %copy-done), kind=kOutput, calls=%fused_computation.1 | convolution fusion | flops 71303168 | bytes 4358144 | tf_op jit(solution)/shard_map/dot_general | solution.py:10
  11.7 0.0 copy-start.4
  11.7 0.0 copy-start.5
  11.7 0.0 all-gather.4.cloned.1.call-update
  11.8 0.0 all-gather.6.cloned.1.call-start
  11.8 0.0 copy-done.1
  11.8 0.0 copy-done.3
  11.8 0.0 copy-done.2
  11.8 2.1 add_convert_fusion
  13.9 0.0 all-gather.6.cloned.1.call-update
  13.9 0.0 copy-done.4
  13.9 0.0 copy-done.5
  14.0 23.5 %all-gather = bf16[16,1,128]{2,1,0:T(2,128)(2,1)S(1)} all-gather(bf16[1,1,128]{2,1,0:T(2,128)(2,1)S(1)} %convert_bitcast_fusion), channel_id=1, replica_groups=mesh['zero'=4,'tp'=4,'shift'=2] {'zero','tp'}, dimensions={0}, use_global_device_ids=true | all-gather | bytes 4352 | tf_op jit(solution)/shard_map/all_gather | solution.py:22
  37.5 0.6 reduce
  38.1 126.2 %all-gather.4.cloned.1.call-done = bf16[2048,2048]{1,0:T(8,128)(2,1)} async-done(((bf16[512,2048]{1,0:T(8,128)(2,1)}), bf16[2048,2048]{1,0:T(8,128)(2,1)}) %all-gather.4.cloned.1.call-update) | async-done | bytes 8388624 | tf_op jit(solution)/shard_map/all_gather | solution.py:18
  164.3 12.4 %copy.15 = bf16[2048,2048]{1,0:T(8,128)(2,1)} copy(bf16[2048,2048]{0,1:T(8,128)(2,1)} %bitcast.9) | data formatting | bytes 16777216
  176.7 137.0 %all-gather.6.cloned.1.call-done = bf16[2048,2048]{1,0:T(8,128)(2,1)} async-done(((bf16[512,2048]{1,0:T(8,128)(2,1)}), bf16[2048,2048]{1,0:T(8,128)(2,1)}) %all-gather.6.cloned.1.call-update) | async-done | bytes 8388624 | tf_op jit(solution)/shard_map/all_gather | solution.py:19
  313.7 12.2 %copy.16 = bf16[2048,2048]{1,0:T(8,128)(2,1)} copy(bf16[2048,2048]{0,1:T(8,128)(2,1)} %bitcast.10) | data formatting | bytes 16777216
  (1 shorter events, 0.0 us)
Async XLA Ops:
  7.2 0.9 copy-start
  7.2 4.6 %copy-start.1 = (bf16[512,2048]{1,0:T(8,128)(2,1)S(1)}, bf16[512,2048]{1,0:T(8,128)(2,1)}, u32[]{:S(2)}) copy-start(bf16[512,2048]{1,0:T(8,128)(2,1)} %param.11) | copy-start | bytes 6291460
  7.2 4.6 %copy-start.3 = (bf16[512,32]{0,1:T(8,128)(2,1)S(1)}, bf16[512,32]{0,1:T(8,128)(2,1)}, u32[]{:S(2)}) copy-start(bf16[512,32]{0,1:T(8,128)(2,1)} %param.12) | copy-start | bytes 98308
  7.2 4.6 %copy-start.2 = (bf16[32,2048]{1,0:T(8,128)(2,1)S(1)}, bf16[32,2048]{1,0:T(8,128)(2,1)}, u32[]{:S(2)}) copy-start(bf16[32,2048]{1,0:T(8,128)(2,1)} %param.13) | copy-start | bytes 393220
  7.2 157.0 %all-gather.4.cloned.1.call-start = ((), (), s32[]{:S(2)}) async-start(), calls=%async_computation | async-start | bytes 10485760 | tf_op jit(solution)/shard_map/all_gather | solution.py:18
  11.7 2.2 copy-start.4
  11.7 2.2 copy-start.5
  11.8 301.9 %all-gather.6.cloned.1.call-start = ((), (), s32[]{:S(2)}) async-start(), calls=%async_computation.1 | async-start | bytes 10485760 | tf_op jit(solution)/shard_map/all_gather | solution.py:19
Sparse Core Ops, SparseCore 0:
  11.9 152.3 all-gather.3
  165.8 147.8 all-gather.5
where the time goes:
time: 333 us
  waiting for transfers between devices  263 us (79%)
  local copies, waits for them, and re-layouts  25.5 us (8%)
  blocking collectives  23.5 us (7%)
  between operations  14.1 us (4%)
  matrix products  5.73 us (2%)
    all_gather x1, waiting for transfers between devices, body(): lax.all_gather(narrow_up, 'zero', axis=0, tiled=True)  137 us
    all_gather x1, waiting for transfers between devices, body(): lax.all_gather(narrow_gate, 'zero', axis=0, tiled=True)  126 us
    unnamed x14, local copies, waits for them, and re-layouts  25.5 us
    all_gather x1, blocking collectives, body(): lax.all_gather((norm_train + norm_step).astype(jnp.bfloat16), ('zero', 't...  23.5 us
  transfers between devices with their start and end apart: 2, of which 2 were waited for; matrix products, arithmetic and copies ran while one was open for 5% of the time, Pallas kernels for 0%

commit v1 on v0

--- a/solution.py
+++ b/solution.py
@@ -4,6 +4,9 @@
 from jax.sharding import PartitionSpec as P
 
 mix_rate = 0.5
+_draft_side = lambda xin: jnp.concatenate(
+    lax.all_to_all(jnp.stack(lax.axis_size("zero") * [xin], axis=0), "zero", 0, 0), axis=0
+)
 
 
 def body(train_gate, low_gate, high_gate, train_up, low_up, high_up, norm_train, norm_step):
@@ -15,7 +18,7 @@
     )
     narrow_gate, narrow_up = (latest_gate.astype(jnp.bfloat16), latest_up.astype(jnp.bfloat16))
     ready_gate, ready_up = (
-        lax.all_gather(narrow_gate, "zero", axis=0, tiled=True),
+        _draft_side(narrow_gate),
         lax.all_gather(narrow_up, "zero", axis=0, tiled=True),
     )
     ready_gate, ready_up = (ready_gate.T, ready_up.T)

time: 333 us -> 396 us (1.19)
  the two profiles are of different devices: /device:TPU:0 before, /device:TPU:13 now
where the time goes in v1:
time: 396 us; the launch traced here: 395 us
  blocking collectives  325 us (82%)
  local copies, waits for them, and re-layouts  43.6 us (11%)
  between operations  14.1 us (4%)
  starting transfers between devices  5.9 us (1%)
  matrix products  5.74 us (1%)
    all_gather x1, blocking collectives, body(): lax.all_gather((norm_train + norm_step).astype(jnp.bfloat16), ('zero', 't...  325 us
    unnamed x14, local copies, waits for them, and re-layouts  25.4 us
    all_to_all x1, local copies, waits for them, and re-layouts, lax.all_to_all(jnp.stack(lax.axis_size('zero') * [xin], axis=0), 'zero',...  11.3 us
  transfers between devices with their start and end apart: 2, of which 0 were waited for; matrix products, arithmetic and copies ran while one was open for 7% of the time, Pallas kernels for 0%

profile of v1, /device:TPU:13, one launch (start us, length us, event | category | flops | bytes accessed | tf_op | source)
XLA Modules:
  0.0 395.1 jit_solution(9445103498093579790)
XLA Ops:
  7.2 0.0 copy-start
  7.2 0.9 copy-done
  8.1 3.7 add_convert_fusion.1
  11.7 2.9 copy.17
  14.6 4.1 %stack.2 = bf16[4,512,2048]{1,2,0:T(8,128)(2,1)} broadcast(bf16[512,2048]{0,1:T(8,128)(2,1)S(1)} %copy.17), dimensions={1,2} | broadcast | bytes 10485760 | tf_op jit(solution)/shard_map/stack | solution.py:8
  18.7 0.0 copy-start.1
  18.7 0.0 copy-start.2
  18.7 0.0 copy-start.3
  18.7 5.9 %all-to-all-start = ((bf16[4,512,2048]{1,2,0:T(8,128)(2,1)}), bf16[4,512,2048]{1,2,0:T(8,128)(2,1)}, u32[]{:S(2)}, u32[]{:S(2)}) async-start(bf16[4,512,2048]{1,2,0:T(8,128)(2,1)} %stack.2), calls=%async_computation | async-start | bytes 16777216 | tf_op jit(solution)/shard_map/all_to_all | solution.py:8
  24.6 0.0 copy-start.4
  24.6 0.0 all-gather.3.cloned.1.call-start
  24.6 0.0 copy-done.1
  24.6 0.0 copy-done.2
  24.6 0.0 copy-done.3
  24.6 2.1 add_convert_fusion
  26.7 0.0 all-gather.3.cloned.1.call-update
  26.7 0.0 copy-done.4
  26.7 0.0 copy-done.5
  26.7 325.1 %all-gather = bf16[16,1,128]{2,1,0:T(2,128)(2,1)S(1)} all-gather(bf16[1,1,128]{2,1,0:T(2,128)(2,1)S(1)} %convert_bitcast_fusion), channel_id=1, replica_groups=mesh['zero'=4,'tp'=4,'shift'=2] {'zero','tp'}, dimensions={0}, use_global_device_ids=true | all-gather | bytes 4352 | tf_op jit(solution)/shard_map/all_gather | solution.py:25
  351.9 0.6 reduce
  352.5 0.0 all-to-all-done
  352.5 11.3 %copy.18 = bf16[4,512,2048]{2,1,0:T(8,128)(2,1)} copy(bf16[4,512,2048]{1,2,0:T(8,128)(2,1)} %all-to-all-done) | data formatting | bytes 16777216 | tf_op jit(solution)/shard_map/all_to_all | solution.py:8
  363.8 12.2 %copy.19 = bf16[2048,2048]{1,0:T(8,128)(2,1)} copy(bf16[2048,2048]{0,1:T(8,128)(2,1)} %bitcast.11) | data formatting | bytes 16777216
  376.1 12.2 %copy.20 = bf16[2048,2048]{1,0:T(8,128)(2,1)} copy(bf16[2048,2048]{0,1:T(8,128)(2,1)} %bitcast.12) | data formatting | bytes 16777216
  (3 shorter events, 0.0 us)
Async XLA Ops:
  7.2 0.9 copy-start
  18.7 5.9 %copy-start.1 = (bf16[512,2048]{1,0:T(8,128)(2,1)S(1)}, bf16[512,2048]{1,0:T(8,128)(2,1)}, u32[]{:S(2)}) copy-start(bf16[512,2048]{1,0:T(8,128)(2,1)} %param.11) | copy-start | bytes 6291460
  18.7 5.9 %copy-start.2 = (bf16[32,2048]{1,0:T(8,128)(2,1)S(1)}, bf16[32,2048]{1,0:T(8,128)(2,1)}, u32[]{:S(2)}) copy-start(bf16[32,2048]{1,0:T(8,128)(2,1)} %param.13) | copy-start | bytes 393220
  18.7 5.9 %copy-start.3 = (bf16[512,32]{0,1:T(8,128)(2,1)S(1)}, bf16[512,32]{0,1:T(8,128)(2,1)}, u32[]{:S(2)}) copy-start(bf16[512,32]{0,1:T(8,128)(2,1)} %param.12) | copy-start | bytes 98308
  18.7 333.8 %all-to-all-start = ((bf16[4,512,2048]{1,2,0:T(8,128)(2,1)}), bf16[4,512,2048]{1,2,0:T(8,128)(2,1)}, u32[]{:S(2)}, u32[]{:S(2)}) async-start(bf16[4,512,2048]{1,2,0:T(8,128)(2,1)} %stack.2), calls=%async_computation | async-start | bytes 16777216 | tf_op jit(solution)/shard_map/all_to_all | solution.py:8
  24.6 2.1 copy-start.4
  24.6 2.1 copy-start.5
  24.6 351.5 %all-gather.3.cloned.1.call-start = ((), (), s32[]{:S(2)}) async-start(), calls=%async_computation.1 | async-start | bytes 10485760 | tf_op jit(solution)/shard_map/all_gather | solution.py:22
Sparse Core Ops, SparseCore 0:
  26.9 304.4 all-gather.2
